TPU v7x, 32 devices: a whole 2x2x4 slice. The times are simulated.
32 devices in a mesh: dp: 8 (over z, x), tensor: 4 (over y, core).
Axes of the slice: x: 2, y: 2, z: 4, core: 2. Of those that a mesh axis runs over, the one named last changes fastest.
Arguments:
- residual_in: float32 [16384, 768], P(('dp', 'tensor')), may hold values from -6 to 6
- out_grad: float32 [16384, 768], P(('dp', 'tensor')), may hold values from -6 to 6
- seq_lengths: int32 [8, 16], P('dp'), may hold values from 0 to 1024, as said below
- timesteps: int32 [8, 16], P('dp'), may hold values from 0 to 1023
- norm_gain: float32 [768], replicated, may hold values from 0.5 to 1.5
- norm_bias: float32 [768], replicated, may hold values from -3 to 3
- qkv_weight: float32 [3, 768, 768], P(None, 'dp', 'tensor'), may hold values from -0.21875 to 0.21875
- proj_weight: float32 [768, 768], P('tensor', 'dp'), may hold values from -0.875 to 0.875
- proj_bias: float32 [768], replicated, may hold values from -2 to 2
- up_weight: float32 [768, 3072], P('dp', 'tensor'), may hold values from -0.21875 to 0.21875
- up_bias: float32 [3072], replicated, may hold values from -3 to 3
- down_weight: float32 [3072, 768], P('tensor', 'dp'), may hold values from -0.109375 to 0.109375
- down_bias: float32 [768], replicated, may hold values from -2 to 2
- time_weight: float32 [128, 2304], replicated, may hold values from -0.5 to 0.5
- time_bias: float32 [2304], replicated, may hold values from -3 to 3
Outputs:
- residual_out: float32 [16384, 768], P(('dp', 'tensor'))
- input_grad: float32 [16384, 768], P(('dp', 'tensor'))
- norm_gain_grad: float32 [768], replicated
- norm_bias_grad: float32 [768], replicated
- qkv_weight_grad: float32 [3, 768, 768], P(None, 'dp', 'tensor')
- proj_weight_grad: float32 [768, 768], P('tensor', 'dp')
- proj_bias_grad: float32 [768], replicated
- up_weight_grad: float32 [768, 3072], P('dp', 'tensor')
- up_bias_grad: float32 [3072], replicated
- down_weight_grad: float32 [3072, 768], P('tensor', 'dp')
- down_bias_grad: float32 [768], replicated
- time_weight_grad: float32 [128, 2304], replicated
- time_bias_grad: float32 [2304], replicated
Inputs may be any that keep to these rules, and one draw needn't show every extreme that they name: `seq_lengths`: row g lists the lengths of the sequences packed in order into the 2048 rows of pack g: the nonzero lengths come first and lie between 128 and 1024, their sum is at most 2048, the rows after it are padding, and every row holds a length of exactly 1024.
All inputs are finite; a program needn't handle non-finite values.
Results may differ from a plain program's by a relative error of at most 0.015.
Values may be sent and summed in bfloat16 or wider, within the bound.
A program may use at most 128 MiB of HBM per device.

v0:
```python
import math
import jax
import jax.numpy as jnp
from jax import lax
from jax.sharding import PartitionSpec as P

HDIM = 64
QBLK = 512
highest = lax.Precision.HIGHEST


def normalize(values):
    center = values - jnp.mean(values, axis=-1, keepdims=True)
    inverse = lax.rsqrt(jnp.mean(center * center, axis=-1, keepdims=True) + 1e-05)
    return (center * inverse, inverse)


def norm_back(grad_in, normed, inverse):
    return inverse * (
        grad_in
        - jnp.mean(grad_in, axis=-1, keepdims=True)
        - normed * jnp.mean(grad_in * normed, axis=-1, keepdims=True)
    )


def pack_info(lengths, row_total):
    row_index = jnp.arange(row_total, dtype=jnp.int32)
    seq_ends = jnp.cumsum(lengths)
    passed = row_index[:, None] >= seq_ends[None, :]
    segment = jnp.sum(passed.astype(jnp.int32), axis=1)
    starts = jnp.sum(jnp.where(passed, lengths[None, :], 0), axis=1)
    return (segment, row_index - starts)


def time_embed(time_index, embed_width):
    half_width = embed_width // 2
    freqs = jnp.exp(-math.log(10000.0) * jnp.arange(half_width, dtype=jnp.float32) / half_width)
    angles = time_index.astype(jnp.float32)[:, None] * freqs[None, :]
    return jnp.concatenate([jnp.cos(angles), jnp.sin(angles)], axis=1)


def rope_tables(positions, head_width):
    half_width = head_width // 2
    inverse = jnp.exp(
        -math.log(10000.0) * jnp.arange(half_width, dtype=jnp.float32) * (2.0 / head_width)
    )
    angles = positions.astype(jnp.float32)[:, None] * inverse[None, :]
    return (jnp.cos(angles)[:, None, :], jnp.sin(angles)[:, None, :])


def rotate(values, cosine, sine_table):
    half_width = values.shape[-1] // 2
    lead_half = values[..., :half_width]
    tail_half = values[..., half_width:]
    return jnp.concatenate(
        [lead_half * cosine - tail_half * sine_table, tail_half * cosine + lead_half * sine_table],
        axis=-1,
    )


def masked_scores(query_block, segment_block, keys_low, segment):
    scores = jnp.einsum("qhd,khd->hqk", query_block, keys_low, preferred_element_type=jnp.float32)
    allowed = segment_block[:, None] == segment[None, :]
    return jnp.where(allowed[None], scores, -1000000000.0)


def gelu_tanh(values):
    return jax.nn.gelu(values, approximate=True)


def shards(
    residual_in,
    out_grad,
    seq_lengths,
    timesteps,
    norm_gain,
    norm_bias,
    qkv_weight,
    proj_weight,
    proj_bias,
    up_weight,
    up_bias,
    down_weight,
    down_bias,
    time_weight,
    time_bias,
):
    row_count = residual_in.shape[0]
    width_model = residual_in.shape[1]
    tensor_size = lax.axis_size("tensor")
    tensor_rank = lax.axis_index("tensor")
    total_rows = row_count * tensor_size
    own_offset = tensor_rank * row_count
    segment, positions = pack_info(seq_lengths[0], total_rows)
    slot_count = seq_lengths.shape[1]
    own_segment = lax.dynamic_slice_in_dim(segment, own_offset, row_count)
    onehot = (own_segment[:, None] == jnp.arange(slot_count, dtype=jnp.int32)[None, :]).astype(
        jnp.float32
    )
    embedded = time_embed(timesteps[0], time_weight.shape[0])
    mod_table = jnp.dot(embedded, time_weight, precision=highest) + time_bias
    modulation = jnp.dot(onehot, mod_table, precision=highest)
    mod_scale = modulation[:, :width_model]
    mod_shift = modulation[:, width_model : 2 * width_model]
    mod_gate = modulation[:, 2 * width_model :]
    gathered_qkv, gathered_proj, gathered_up, gathered_down = (
        lax.all_gather(qkv_weight.astype(jnp.bfloat16), "dp", axis=1, tiled=True),
        lax.all_gather(proj_weight.astype(jnp.bfloat16), "dp", axis=1, tiled=True),
        lax.all_gather(up_weight.astype(jnp.bfloat16), "dp", axis=0, tiled=True),
        lax.all_gather(down_weight.astype(jnp.bfloat16), "dp", axis=1, tiled=True),
    )
    local_heads = gathered_qkv.shape[2] // HDIM
    local_units = gathered_up.shape[1]
    normed_in, inverse_in = normalize(residual_in)
    normed_low = (normed_in * norm_gain + norm_bias).astype(jnp.bfloat16)
    normed_full = lax.all_gather(normed_low, "tensor", axis=0, tiled=True)
    projected = jnp.einsum(
        "td,cde->cte", normed_full, gathered_qkv, preferred_element_type=jnp.float32
    )
    cosine, sine_table = rope_tables(positions, HDIM)
    head_scale = 1.0 / math.sqrt(HDIM)
    queries_low = (
        rotate(projected[0].reshape(total_rows, local_heads, HDIM), cosine, sine_table) * head_scale
    ).astype(jnp.bfloat16)
    keys_low = rotate(
        projected[1].reshape(total_rows, local_heads, HDIM), cosine, sine_table
    ).astype(jnp.bfloat16)
    values_low = projected[2].reshape(total_rows, local_heads, HDIM).astype(jnp.bfloat16)
    block_count = total_rows // QBLK
    query_blocks = queries_low.reshape(block_count, QBLK, local_heads, HDIM)
    segment_blocks = segment.reshape(block_count, QBLK)

    def forward_block(block_item):
        query_block, segment_block = block_item
        scores = masked_scores(query_block, segment_block, keys_low, segment)
        row_max = jnp.max(scores, axis=-1, keepdims=True)
        exponent = jnp.exp(scores - row_max)
        row_total = jnp.sum(exponent, axis=-1, keepdims=True)
        soft_weights = exponent / row_total
        mixed = jnp.einsum(
            "hqk,khd->qhd",
            soft_weights.astype(jnp.bfloat16),
            values_low,
            preferred_element_type=jnp.float32,
        )
        return (mixed.astype(jnp.bfloat16), (row_max + jnp.log(row_total))[..., 0])

    mixed_blocks, log_totals = lax.map(forward_block, (query_blocks, segment_blocks))
    mixed_flat = mixed_blocks.reshape(total_rows, local_heads * HDIM)
    attention = lax.psum_scatter(
        jnp.dot(mixed_flat, gathered_proj, preferred_element_type=jnp.float32).astype(jnp.bfloat16),
        "tensor",
        scatter_dimension=0,
        tiled=True,
    ).astype(jnp.float32)
    hidden = residual_in + attention + proj_bias
    hidden_normed, inverse_hidden = normalize(hidden)
    modulated_low = (hidden_normed * (1.0 + mod_scale) + mod_shift).astype(jnp.bfloat16)
    branch_grad = out_grad * mod_gate
    modulated_full = lax.all_gather(modulated_low, "tensor", axis=0, tiled=True)
    up_bias_own = lax.dynamic_slice_in_dim(up_bias, tensor_rank * local_units, local_units)
    pre_act = jnp.dot(modulated_full, gathered_up, preferred_element_type=jnp.float32) + up_bias_own
    active, gelu_pullback = jax.vjp(gelu_tanh, pre_act)
    active_low = active.astype(jnp.bfloat16)
    down_sum = lax.psum_scatter(
        jnp.dot(active_low, gathered_down, preferred_element_type=jnp.float32).astype(jnp.bfloat16),
        "tensor",
        scatter_dimension=0,
        tiled=True,
    ).astype(jnp.float32)
    branch = down_sum + down_bias
    residual_out = hidden + mod_gate * branch
    gate_grad = out_grad * branch
    branch_full = lax.all_gather(branch_grad.astype(jnp.bfloat16), "tensor", axis=0, tiled=True)
    down_part = lax.dot_general(
        active_low, branch_full, (((0,), (0,)), ((), ())), preferred_element_type=jnp.float32
    )
    active_grad = lax.dot_general(
        branch_full, gathered_down, (((1,), (1,)), ((), ())), preferred_element_type=jnp.float32
    )
    pre_grad = gelu_pullback(active_grad)[0].astype(jnp.bfloat16)
    up_bias_own_part = jnp.sum(pre_grad, axis=0, dtype=jnp.float32)
    up_bias_part = lax.dynamic_update_slice_in_dim(
        jnp.zeros(up_bias.shape, jnp.float32), up_bias_own_part, tensor_rank * local_units, 0
    )
    up_part = lax.dot_general(
        modulated_full, pre_grad, (((0,), (0,)), ((), ())), preferred_element_type=jnp.float32
    )
    modulated_grad = lax.psum_scatter(
        lax.dot_general(
            pre_grad, gathered_up, (((1,), (1,)), ((), ())), preferred_element_type=jnp.float32
        ).astype(jnp.bfloat16),
        "tensor",
        scatter_dimension=0,
        tiled=True,
    ).astype(jnp.float32)
    down_bias_part = jnp.sum(branch_grad, axis=0)
    scale_grad = modulated_grad * hidden_normed
    hidden_norm_grad = modulated_grad * (1.0 + mod_scale)
    hidden_grad = out_grad + norm_back(hidden_norm_grad, hidden_normed, inverse_hidden)
    mod_grad = jnp.concatenate([scale_grad, modulated_grad, gate_grad], axis=1)
    mod_seq_grad = lax.dot_general(onehot, mod_grad, (((0,), (0,)), ((), ())), precision=highest)
    time_weight_part = lax.dot_general(
        embedded, mod_seq_grad, (((0,), (0,)), ((), ())), precision=highest
    )
    time_bias_part = jnp.sum(mod_seq_grad, axis=0)
    proj_bias_part = jnp.sum(hidden_grad, axis=0)
    hidden_full = lax.all_gather(hidden_grad.astype(jnp.bfloat16), "tensor", axis=0, tiled=True)
    proj_part = lax.dot_general(
        mixed_flat, hidden_full, (((0,), (0,)), ((), ())), preferred_element_type=jnp.float32
    )
    mixed_grad = lax.dot_general(
        hidden_full, gathered_proj, (((1,), (1,)), ((), ())), preferred_element_type=jnp.float32
    )
    grad_blocks = mixed_grad.astype(jnp.bfloat16).reshape(block_count, QBLK, local_heads, HDIM)

    def backward_block(carried, block_item):
        key_sum, value_sum = carried
        query_block, segment_block, log_block, grad_block = block_item
        scores = masked_scores(query_block, segment_block, keys_low, segment)
        soft_weights = jnp.exp(scores - log_block[:, :, None])
        prob_grad = jnp.einsum(
            "qhd,khd->hqk", grad_block, values_low, preferred_element_type=jnp.float32
        )
        row_inner = jnp.sum(soft_weights * prob_grad, axis=-1, keepdims=True)
        score_grad = (soft_weights * (prob_grad - row_inner)).astype(jnp.bfloat16)
        query_grad = jnp.einsum(
            "hqk,khd->qhd", score_grad, keys_low, preferred_element_type=jnp.float32
        )
        key_sum = key_sum + jnp.einsum(
            "hqk,qhd->khd", score_grad, query_block, preferred_element_type=jnp.float32
        )
        value_sum = value_sum + jnp.einsum(
            "hqk,qhd->khd",
            soft_weights.astype(jnp.bfloat16),
            grad_block,
            preferred_element_type=jnp.float32,
        )
        return ((key_sum, value_sum), query_grad)

    empty_grad = jnp.zeros((total_rows, local_heads, HDIM), jnp.float32)
    (key_grad, value_grad), query_grads = lax.scan(
        backward_block,
        (empty_grad, empty_grad),
        (query_blocks, segment_blocks, log_totals, grad_blocks),
    )
    query_grad_all = query_grads.reshape(total_rows, local_heads, HDIM)
    query_raw_grad = rotate(query_grad_all * head_scale, cosine, -sine_table)
    key_raw_grad = rotate(key_grad, cosine, -sine_table)
    qkv_grad = (
        jnp.stack([query_raw_grad, key_raw_grad, value_grad])
        .reshape(3, total_rows, local_heads * HDIM)
        .astype(jnp.bfloat16)
    )
    qkv_part = jnp.einsum("td,cte->cde", normed_full, qkv_grad, preferred_element_type=jnp.float32)
    normed_grad = lax.psum_scatter(
        jnp.einsum(
            "cte,cde->td", qkv_grad, gathered_qkv, preferred_element_type=jnp.float32
        ).astype(jnp.bfloat16),
        "tensor",
        scatter_dimension=0,
        tiled=True,
    ).astype(jnp.float32)
    gain_part = jnp.sum(normed_grad * normed_in, axis=0)
    bias_part = jnp.sum(normed_grad, axis=0)
    input_grad = hidden_grad + norm_back(normed_grad * norm_gain, normed_in, inverse_in)
    grad_qkv, grad_proj, grad_up, grad_down = (
        lax.psum_scatter(qkv_part, "dp", scatter_dimension=1, tiled=True),
        lax.psum_scatter(proj_part, "dp", scatter_dimension=1, tiled=True),
        lax.psum_scatter(up_part, "dp", scatter_dimension=0, tiled=True),
        lax.psum_scatter(down_part, "dp", scatter_dimension=1, tiled=True),
    )
    small_sums = lax.psum(
        (
            gain_part,
            bias_part,
            proj_bias_part,
            up_bias_part,
            down_bias_part,
            time_weight_part,
            time_bias_part,
        ),
        ("dp", "tensor"),
    )
    return (
        residual_out,
        input_grad,
        small_sums[0],
        small_sums[1],
        grad_qkv,
        grad_proj,
        small_sums[2],
        grad_up,
        small_sums[3],
        grad_down,
        small_sums[4],
        small_sums[5],
        small_sums[6],
    )


def solution(mesh):
    in_specs = (
        P(("dp", "tensor"), None),
        P(("dp", "tensor"), None),
        P("dp", None),
        P("dp", None),
        P(),
        P(),
        P(None, "dp", "tensor"),
        P("tensor", "dp"),
        P(),
        P("dp", "tensor"),
        P(),
        P("tensor", "dp"),
        P(),
        P(),
        P(),
    )
    out_specs = (
        P(("dp", "tensor"), None),
        P(("dp", "tensor"), None),
        P(),
        P(),
        P(None, "dp", "tensor"),
        P("tensor", "dp"),
        P(),
        P("dp", "tensor"),
        P(),
        P("tensor", "dp"),
        P(),
        P(),
        P(),
    )
    return jax.shard_map(shards, mesh=mesh, in_specs=in_specs, out_specs=out_specs, check_vma=False)
```

profile of v0, /device:TPU:0, one launch (start us, length us, event | category | flops | bytes accessed | tf_op | source)
XLA Modules:
  0.0 983.2 jit_solution(7752783415744753247)
XLA Ops:
  12.9 40.6 %all_gather.25 = bf16[3,768,192]{2,0,1:T(4,128)(2,1)} all-gather(bf16[3,96,192]{2,0,1:T(4,128)(2,1)S(1)} %copy.65), channel_id=1, replica_groups=mesh['dp'=8,'tensor'=4] {'dp'}, dimensions={1}, use_global_device_ids=true | all-gather | bytes 995328 | tf_op jit(solution)/shard_map/all_gather | solution.py:107
  57.0 33.0 %all_gather.26 = bf16[192,768]{0,1:T(8,128)(2,1)} all-gather(bf16[192,96]{0,1:T(8,128)(2,1)S(1)} %copy.69), channel_id=1, replica_groups=mesh['dp'=8,'tensor'=4] {'dp'}, dimensions={1}, use_global_device_ids=true | all-gather | bytes 331776 | tf_op jit(solution)/shard_map/all_gather | solution.py:108
  106.1 95.3 %while.27 = (s32[]{:T(128)}, bf16[4,512,3,64]{1,3,2,0:T(8,128)(2,1)}, f32[4,3,512]{2,1,0:T(4,128)}, s32[4,512]{1,0:T(4,128)S(1)}, s32[2048]{0:T(1024)S(1)}, /*in...) while((s32[]{:T(128)}, ...), condition=%wide.region_8.9_spmd, body=%wide.region_5.8_spmd.sunk | while | flops 834763264 | bytes 47120528 | solution.py:148
  114.6 7.8 fusion.140
  185.8 7.8 fusion.140
  218.0 26.7 %reduce-scatter.13.cloned.1.call-done = bf16[512,768]{1,0:T(8,128)(2,1)} async-done(((bf16[2048,768]{1,0:T(8,128)(2,1)}), bf16[512,768]{1,0:T(8,128)(2,1)}) %reduce-scatter.13.cloned.1.call-update) | async-done | bytes 786448 | tf_op jit(solution)/shard_map/reduce_scatter | solution.py:150
  252.9 27.2 %all-gather.9.cloned.1.call-done = bf16[2048,768]{1,0:T(8,128)(2,1)} async-done(((bf16[512,768]{1,0:T(8,128)(2,1)}), bf16[2048,768]{1,0:T(8,128)(2,1)}) %all-gather.9.cloned.1.call-update) | async-done | bytes 3145744 | tf_op jit(solution)/shard_map/all_gather | solution.py:160
  287.6 36.0 %all-gather.13.cloned.1.call-done = bf16[768,768]{0,1:T(8,128)(2,1)} async-done(((bf16[768,96]{0,1:T(8,128)(2,1)}), bf16[768,768]{0,1:T(8,128)(2,1)}) %all-gather.13.cloned.1.call-update) | async-done | bytes 1179664 | tf_op jit(solution)/shard_map/all_gather | solution.py:110
  323.6 28.9 %all-gather.15.cloned.1.call-done = bf16[2048,768]{1,0:T(8,128)(2,1)} async-done(((bf16[512,768]{1,0:T(8,128)(2,1)}), bf16[2048,768]{1,0:T(8,128)(2,1)}) %all-gather.15.cloned.1.call-update) | async-done | bytes 3145744 | tf_op jit(solution)/shard_map/all_gather | solution.py:174
  352.6 10.8 %convert_reduce_fusion = (f32[768]{0:T(1024)}, bf16[2048,768]{1,0:T(8,128)(2,1)S(1)}, bf16[2048,768]{1,0:T(8,128)(2,1)}) fusion(f32[2048,768]{1,0:T(8,128)} %fusion.88, f32[768]{0:T(1024)S(1)} %dynamic_slice.28, bf16[2048,768]{1,0:T(8,128)(2,1)} %all-gather.15.cloned.1.call-done, bf16[768,768]{0,1:T(8,128)(2,1)} %all-gather.13.cloned.1.call-done), kind=kOutput, calls=%fused_computation.57 | convolution fusion | flops 2455239936 | bytes 16914432 | tf_op jit(solution)/shard_map/dot_general | solution.py:178
  376.6 30.5 %reduce-scatter.17.cloned.1.call-done = bf16[512,768]{1,0:T(8,128)(2,1)} async-done(((bf16[2048,768]{1,0:T(8,128)(2,1)}), bf16[512,768]{1,0:T(8,128)(2,1)}) %reduce-scatter.17.cloned.1.call-update) | async-done | bytes 786448 | tf_op jit(solution)/shard_map/reduce_scatter | solution.py:189
  411.1 36.4 %reduce-scatter.15.cloned.1.call-done = bf16[512,768]{1,0:T(8,128)(2,1)} async-done(((bf16[2048,768]{1,0:T(8,128)(2,1)}), bf16[512,768]{1,0:T(8,128)(2,1)}) %reduce-scatter.15.cloned.1.call-update) | async-done | bytes 786448 | tf_op jit(solution)/shard_map/reduce_scatter | solution.py:165
  454.8 28.4 %all-gather.17.cloned.1.call-done = bf16[2048,768]{1,0:T(8,128)(2,1)} async-done(((bf16[512,768]{1,0:T(8,128)(2,1)}), bf16[2048,768]{1,0:T(8,128)(2,1)}) %all-gather.17.cloned.1.call-update) | async-done | bytes 3145744 | tf_op jit(solution)/shard_map/all_gather | solution.py:208
  487.0 157.7 %while.28 = (s32[]{:T(128)}, f32[2048,3,64]{0,2,1:T(8,128)}, f32[2048,3,64]{0,2,1:T(8,128)}, f32[4,512,3,64]{1,0,3,2:T(4,128)}, bf16[4,512,3,64]{1,3,2,0:T(8,128...) while((s32[]{:T(128)}, f32[2048,3,64]{0,2,1:T(8,128)}, ...), condition=%wide.region_18.19_spmd.clone, body=%wide.region_16.18_spmd.clone.sunk | while | flops 2053634560 | bytes 151972176 | solution.py:242
  516.4 8.6 dynamic_update_slice.24
  556.3 8.6 dynamic_update_slice.24
  596.1 8.6 dynamic_update_slice.24
  635.9 8.6 dynamic_update_slice.24
  696.3 19.6 %reduce-scatter.27.cloned.1.call-done = f32[96,192]{1,0:T(8,128)} async-done(((f32[768,192]{1,0:T(8,128)}), f32[96,192]{1,0:T(8,128)}) %reduce-scatter.27.cloned.1.call-update) | async-done | bytes 73744
  717.5 68.3 %reduce-scatter.25.cloned.1.call-done = f32[96,576]{1,0:T(8,128)} async-done(((f32[768,576]{1,0:T(8,128)}), f32[96,576]{1,0:T(8,128)}) %reduce-scatter.25.cloned.1.call-update) | async-done | bytes 221200
  787.7 37.6 %reduce-scatter.19.cloned.1.call-done = bf16[512,768]{1,0:T(8,128)(2,1)} async-done(((bf16[2048,768]{1,0:T(8,128)(2,1)}), bf16[512,768]{1,0:T(8,128)(2,1)}) %reduce-scatter.19.cloned.1.call-update) | async-done | bytes 786448 | tf_op jit(solution)/shard_map/reduce_scatter | solution.py:256
  827.8 41.3 %all-reduce = (f32[768]{0:T(1024)}, f32[768]{0:T(1024)}, f32[768]{0:T(1024)}, f32[3072]{0:T(1024)}, f32[768]{0:T(1024)}, /*index=5*/f32[2304]{0:T(1024)}) all-reduce(f32[768]{0:T(1024)S(1)} %get-tuple-element.311, f32[768]{0:T(1024)S(1)} %get-tuple-element.314, ...), channel_id=1, replica_groups=mesh['dp'=8,'tensor'=4] {'dp','tensor'}, use_global_device_ids=true, to_apply=%region_23.24 | all-reduce | flops 8448 | bytes 67584 | tf_op jit(solution)/shard_map/psum | solution.py:273
  872.3 27.9 %reduce-scatter.21.cloned.1.call-done = f32[96,768]{1,0:T(8,128)} async-done(((f32[768,768]{1,0:T(8,128)}), f32[96,768]{1,0:T(8,128)}) %reduce-scatter.21.cloned.1.call-update) | async-done | bytes 294928 | tf_op jit(solution)/shard_map/reduce_scatter | solution.py:270
  900.2 73.0 %reduce-scatter.23.cloned.1.call-done = f32[768,96]{0,1:T(8,128)} async-done(((f32[768,768]{0,1:T(8,128)}), f32[768,96]{0,1:T(8,128)}) %reduce-scatter.23.cloned.1.call-update) | async-done | bytes 294928 | tf_op jit(solution)/shard_map/reduce_scatter | solution.py:271
  (341 shorter events, 349.4 us)
Async XLA Ops:
  8.0 204.3 %copy-start = (f32[128,2304]{1,0:T(8,128)S(1)}, f32[128,2304]{1,0:T(8,128)}, u32[]{:S(2)}) copy-start(f32[128,2304]{1,0:T(8,128)} %param.32) | copy-start | bytes 3538948
  8.1 83.6 %all-gather.7.cloned.1.call-start = ((), (), s32[]{:S(2)}) async-start(), calls=%async_computation.8 | async-start | bytes 3932160 | tf_op jit(solution)/shard_map/all_gather | solution.py:116
  11.6 233.2 %reduce-scatter.13.cloned.1.call-start = ((), (), s32[]{:S(2)}) async-start(), calls=%async_computation.9 | async-start | bytes 3932160 | tf_op jit(solution)/shard_map/reduce_scatter | solution.py:150
  206.9 46.0 %all-gather.11.cloned.1.call-start = ((), (), s32[]{:S(2)}) async-start(), calls=%async_computation.11 | async-start | bytes 1327104 | tf_op jit(solution)/shard_map/all_gather | solution.py:109
  208.6 71.5 %all-gather.9.cloned.1.call-start = ((), (), s32[]{:S(2)}) async-start(), calls=%async_computation.10 | async-start | bytes 3932160 | tf_op jit(solution)/shard_map/all_gather | solution.py:160
  250.6 73.1 %all-gather.13.cloned.1.call-start = ((), (), s32[]{:S(2)}) async-start(), calls=%async_computation.12 | async-start | bytes 1327104 | tf_op jit(solution)/shard_map/all_gather | solution.py:110
  251.3 101.2 %all-gather.15.cloned.1.call-start = ((), (), s32[]{:S(2)}) async-start(), calls=%async_computation.14 | async-start | bytes 3932160 | tf_op jit(solution)/shard_map/all_gather | solution.py:174
  252.1 155.1 %reduce-scatter.17.cloned.1.call-start = ((), (), s32[]{:S(2)}) async-start(), calls=%async_computation.15 | async-start | bytes 3932160 | tf_op jit(solution)/shard_map/reduce_scatter | solution.py:189
  287.6 77.4 %copy-start.57 = (bf16[768,768]{1,0:T(8,128)(2,1)S(1)}, bf16[768,768]{1,0:T(8,128)(2,1)}, u32[]{:S(2)}) copy-start(bf16[768,768]{1,0:T(8,128)(2,1)} %all-gather.11.cloned.1.call-done) | copy-start | bytes 3538948
  369.1 78.3 %reduce-scatter.15.cloned.1.call-start = ((), (), s32[]{:S(2)}) async-start(), calls=%async_computation.13 | async-start | bytes 3932160 | tf_op jit(solution)/shard_map/reduce_scatter | solution.py:165
  376.6 106.6 %all-gather.17.cloned.1.call-start = ((), (), s32[]{:S(2)}) async-start(), calls=%async_computation.16 | async-start | bytes 3932160 | tf_op jit(solution)/shard_map/all_gather | solution.py:208
  454.7 261.2 %reduce-scatter.27.cloned.1.call-start = ((), (), s32[]{:S(2)}) async-start(), calls=%async_computation.22 | async-start | bytes 884736
  652.1 133.7 %reduce-scatter.25.cloned.1.call-start = ((), (), s32[]{:S(2)}) async-start(), calls=%async_computation.21 | async-start | bytes 2211840
  666.9 158.4 %reduce-scatter.19.cloned.1.call-start = ((), (), s32[]{:S(2)}) async-start(), calls=%async_computation.17 | async-start | bytes 3932160 | tf_op jit(solution)/shard_map/reduce_scatter | solution.py:256
  674.0 226.3 %reduce-scatter.21.cloned.1.call-start = ((), (), s32[]{:S(2)}) async-start(), calls=%async_computation.18 | async-start | bytes 2654208 | tf_op jit(solution)/shard_map/reduce_scatter | solution.py:270
  681.9 291.4 %reduce-scatter.23.cloned.1.call-start = ((), (), s32[]{:S(2)}) async-start(), calls=%async_computation.19 | async-start | bytes 2654208 | tf_op jit(solution)/shard_map/reduce_scatter | solution.py:271
  689.2 284.1 %all-reduce.3.cloned.1.call-start = ((), (), s32[]{:S(2)}) async-start(), calls=%async_computation.20 | async-start | bytes 2359296 | tf_op jit(solution)/shard_map/psum | solution.py:273
  694.0 131.3 %copy-start.8 = (f32[512,768]{1,0:T(8,128)S(1)}, f32[512,768]{1,0:T(8,128)}, u32[]{:S(2)}) copy-start(f32[512,768]{1,0:T(8,128)} %param.19) | copy-start | bytes 4718596
  694.0 131.3 %copy-start.40 = (f32[512]{0:T(512)S(1)}, f32[512]{0:T(512)}, u32[]{:S(2)}) copy-start(f32[512]{0:T(512)} %copy-done.39) | copy-start | bytes 6148
  694.0 131.2 %copy-start.42 = (f32[768]{0:T(1024)S(1)}, f32[768]{0:T(1024)}, u32[]{:S(2)}) copy-start(f32[768]{0:T(1024)} %param.23) | copy-start | bytes 9220
  694.0 131.2 %copy-start.44 = (f32[512]{0:T(512)S(1)}, f32[512]{0:T(512)}, u32[]{:S(2)}) copy-start(f32[512]{0:T(512)} %copy-done.43) | copy-start | bytes 6148
  717.5 110.3 %copy-start.46 = (f32[768]{0:T(1024)S(1)}, f32[768]{0:T(1024)}, u32[]{:S(2)}) copy-start(f32[768]{0:T(1024)} %get-tuple-element.310) | copy-start | bytes 9220
  717.5 110.3 %copy-start.47 = (f32[768]{0:T(1024)S(1)}, f32[768]{0:T(1024)}, u32[]{:S(2)}) copy-start(f32[768]{0:T(1024)} %get-tuple-element.363) | copy-start | bytes 9220
  869.1 106.5 %copy-start.1 = (f32[128,2304]{1,0:T(8,128)S(1)}, f32[128,2304]{1,0:T(8,128)}, u32[]{:S(2)}) copy-start(f32[128,2304]{1,0:T(8,128)} %param.32) | copy-start | bytes 3538948
  (72 other events, 567.9 us)
Sparse Core Ops, SparseCore 0:
  11.7 31.2 all-gather.6
  207.0 37.6 reduce-scatter.12
  369.2 37.8 reduce-scatter.16
  409.5 37.8 reduce-scatter.14
  696.4 151.9 all-reduce.2
Sparse Core Ops, SparseCore 1:
  210.2 41.1 all-gather.10
  253.3 26.7 all-gather.8
  282.2 41.4 all-gather.12
  325.8 26.7 all-gather.14
  454.8 28.3 all-gather.16
  652.2 63.6 reduce-scatter.26
  719.2 66.5 reduce-scatter.24
  788.2 37.0 reduce-scatter.18
  829.2 71.0 reduce-scatter.20
  904.3 68.9 reduce-scatter.22
where the time goes:
time: 991 us; the launch traced here: 983 us
  waiting for transfers between devices  441 us (45%)
  matrix products  226 us (23%)
  blocking collectives  115 us (12%)
  other arithmetic  102 us (10%)
  local copies, waits for them, and re-layouts  79.7 us (8%)
  between operations  16.4 us (2%)
    unnamed x17, waiting for transfers between devices  88.8 us
    reduce_scatter x1, waiting for transfers between devices, shards(): lax.psum_scatter(down_part, 'dp', scatter_dimension=1, tiled=True)  73 us
    dot_general x8, matrix products, masked_scores(): jnp.einsum('qhd,khd->hqk', query_block, keys_low, preferred_element_type=...  42.3 us
    psum x1, blocking collectives, shards(): lax.psum((gain_part, bias_part, proj_bias_part, up_bias_part, down_bias_p...  41.3 us
    all_gather x1, blocking collectives, shards(): lax.all_gather(qkv_weight.astype(jnp.bfloat16), 'dp', axis=1, tiled=True)  40.6 us
    reduce_scatter x1, waiting for transfers between devices, shards(): lax.psum_scatter(jnp.einsum('cte,cde->td', qkv_grad, gathered_qkv, prefer...  37.6 us
    reduce_scatter x1, waiting for transfers between devices, shards(): lax.psum_scatter(jnp.dot(active_low, gathered_down, preferred_element_typ...  36.4 us
    dynamic_update_slice x8, local copies, waits for them, and re-layouts, shards(): lax.scan(backward_block, (empty_grad, empty_grad), (query_blocks, segment...  36 us
  transfers between devices with their start and end apart: 15, of which 12 were waited for; matrix products, arithmetic and copies ran while one was open for 9% of the time, Pallas kernels for 0%

commit v1 on v0

--- a/solution.py
+++ b/solution.py
@@ -157,7 +157,30 @@
     hidden_normed, inverse_hidden = normalize(hidden)
     modulated_low = (hidden_normed * (1.0 + mod_scale) + mod_shift).astype(jnp.bfloat16)
     branch_grad = out_grad * mod_gate
-    modulated_full = lax.all_gather(modulated_low, "tensor", axis=0, tiled=True)
+    tile_out, arr_now, spare = (
+        jax.lax.axis_size("tensor"),
+        jax.lax.axis_index("tensor"),
+        modulated_low.shape[0],
+    )
+    seen = [t * tile_out if kk == 0 else t for kk, t in enumerate(modulated_low.shape)]
+    modulated_full = lax.dynamic_update_slice_in_dim(
+        jnp.zeros(seen, modulated_low.dtype), modulated_low, arr_now * spare, axis=0
+    )
+    vec_out = x_now = modulated_low
+    for ix in range(1, tile_out // 2 + 1):
+        vec_out = jax.lax.ppermute(
+            vec_out, "tensor", [(kk, (kk + 1) % tile_out) for kk in range(tile_out)]
+        )
+        modulated_full = lax.dynamic_update_slice_in_dim(
+            modulated_full, vec_out, (arr_now - ix) % tile_out * spare, axis=0
+        )
+        if 2 * ix < tile_out:
+            x_now = jax.lax.ppermute(
+                x_now, "tensor", [(kk, (kk - 1) % tile_out) for kk in range(tile_out)]
+            )
+            modulated_full = lax.dynamic_update_slice_in_dim(
+                modulated_full, x_now, (arr_now + ix) % tile_out * spare, axis=0
+            )
     up_bias_own = lax.dynamic_slice_in_dim(up_bias, tensor_rank * local_units, local_units)
     pre_act = jnp.dot(modulated_full, gathered_up, preferred_element_type=jnp.float32) + up_bias_own
     active, gelu_pullback = jax.vjp(gelu_tanh, pre_act)

time: 991 us -> 967 us (0.976)
  waiting for transfers between devices: 441 us -> 423 us
    all_gather x1, waiting for transfers between devices: 36 us -> 0.01 us  [shards(): lax.all_gather(down_weight.astype(jnp.bfloat16), 'dp', axis=1, tiled=True)]
    all_gather x1, waiting for transfers between devices: 0.01 us -> 34 us  [shards(): lax.all_gather(up_weight.astype(jnp.bfloat16), 'dp', axis=0, tiled=True)]
    all_gather x1 -> x0, waiting for transfers between devices: 27.2 us -> none  [shards(): modulated_full = lax.all_gather(modulated_low, 'tensor', axis=0, tiled=True)]
    ppermute x0 -> x3, waiting for transfers between devices: none -> 26.4 us  [the longest x2 26.4 us: shards(): jax.lax.ppermute(vec_out, 'tensor', [(kk, (kk + 1) % tile_out) for kk in...]
    all_gather x1, waiting for transfers between devices: 28.9 us -> 12.1 us  [shards(): lax.all_gather(branch_grad.astype(jnp.bfloat16), 'tensor', axis=0, tiled=...]
    unnamed x17 -> x16, waiting for transfers between devices: 88.8 us -> 92 us
    unnamed x115 -> x125, local copies, waits for them, and re-layouts: 25.8 us -> 25.8 us
  transfers between devices with their start and end apart: 15 -> 17, of which waited for: 12 -> 12; matrix products, arithmetic and copies ran while one was open for 9% -> 9% of each run, Pallas kernels for 0% -> 0%
where the time goes in v1:
time: 967 us; the launch traced here: 959 us
  waiting for transfers between devices  423 us (44%)
  matrix products  224 us (23%)
  blocking collectives  112 us (12%)
  other arithmetic  97.6 us (10%)
  local copies, waits for them, and re-layouts  82.5 us (9%)
  between operations  16.5 us (2%)
    unnamed x16, waiting for transfers between devices  92 us
    reduce_scatter x1, waiting for transfers between devices, shards(): lax.psum_scatter(down_part, 'dp', scatter_dimension=1, tiled=True)  73 us
    dot_general x8, matrix products, masked_scores(): jnp.einsum('qhd,khd->hqk', query_block, keys_low, preferred_element_type=...  42.5 us
    psum x1, blocking collectives, shards(): lax.psum((gain_part, bias_part, proj_bias_part, up_bias_part, down_bias_p...  41.5 us
    all_gather x1, blocking collectives, shards(): lax.all_gather(qkv_weight.astype(jnp.bfloat16), 'dp', axis=1, tiled=True)  38.8 us
    reduce_scatter x1, waiting for transfers between devices, shards(): lax.psum_scatter(jnp.einsum('cte,cde->td', qkv_grad, gathered_qkv, prefer...  37.7 us
    reduce_scatter x1, waiting for transfers between devices, shards(): lax.psum_scatter(jnp.dot(active_low, gathered_down, preferred_element_typ...  36.4 us
    dynamic_update_slice x8, local copies, waits for them, and re-layouts, shards(): lax.scan(backward_block, (empty_grad, empty_grad), (query_blocks, segment...  36 us
  transfers between devices with their start and end apart: 17, of which 12 were waited for; matrix products, arithmetic and copies ran while one was open for 9% of the time, Pallas kernels for 0%

profile of v1, /device:TPU:0, one launch (start us, length us, event | category | flops | bytes accessed | tf_op | source)
XLA Modules:
  0.0 959.2 jit_solution(9266808771368937514)
XLA Ops:
  12.9 38.8 %all_gather.22 = bf16[3,768,192]{2,0,1:T(4,128)(2,1)S(1)} all-gather(bf16[3,96,192]{2,0,1:T(4,128)(2,1)S(1)} %copy.65), channel_id=1, replica_groups=mesh['dp'=8,'tensor'=4] {'dp'}, dimensions={1}, use_global_device_ids=true | all-gather | bytes 995328 | tf_op jit(solution)/shard_map/all_gather | solution.py:107
  53.8 31.1 %all_gather.23 = bf16[192,768]{0,1:T(8,128)(2,1)S(1)} all-gather(bf16[192,96]{0,1:T(8,128)(2,1)S(1)} %copy.69), channel_id=1, replica_groups=mesh['dp'=8,'tensor'=4] {'dp'}, dimensions={1}, use_global_device_ids=true | all-gather | bytes 331776 | tf_op jit(solution)/shard_map/all_gather | solution.py:108
  99.9 95.0 %while.27 = (s32[]{:T(128)}, bf16[4,512,3,64]{1,3,2,0:T(8,128)(2,1)}, f32[4,3,512]{2,1,0:T(4,128)}, s32[4,512]{1,0:T(4,128)S(1)}, s32[2048]{0:T(1024)S(1)}, /*in...) while((s32[]{:T(128)}, ...), condition=%wide.region_8.9_spmd, body=%wide.region_5.8_spmd.sunk | while | flops 834763264 | bytes 43974772 | solution.py:148
  108.4 7.8 fusion.141
  132.1 7.8 fusion.141
  210.1 27.4 %reduce-scatter.13.cloned.1.call-done = bf16[512,768]{1,0:T(8,128)(2,1)} async-done(((bf16[2048,768]{1,0:T(8,128)(2,1)}), bf16[512,768]{1,0:T(8,128)(2,1)}) %reduce-scatter.13.cloned.1.call-update) | async-done | bytes 786448 | tf_op jit(solution)/shard_map/reduce_scatter | solution.py:150
  247.2 26.4 %collective-permute-done = bf16[512,768]{1,0:T(8,128)(2,1)S(1)} collective-permute-done((bf16[512,768]{1,0:T(8,128)(2,1)}, bf16[512,768]{1,0:T(8,128)(2,1)S(1)}, u32[]{:S(2)}, u32[]{:S(2)}) %collective-permute-start) | collective-permute-done | bytes 786464 | tf_op jit(solution)/shard_map/ppermute | solution.py:171
  273.5 12.1 %all-gather.12.cloned.1.call-done = bf16[2048,768]{1,0:T(8,128)(2,1)} async-done(((bf16[512,768]{1,0:T(8,128)(2,1)}), bf16[2048,768]{1,0:T(8,128)(2,1)}) %all-gather.12.cloned.1.call-update) | async-done | bytes 3145744 | tf_op jit(solution)/shard_map/all_gather | solution.py:197
  296.0 34.0 %all-gather.8.cloned.1.call-done = bf16[768,768]{1,0:T(8,128)(2,1)} async-done(((bf16[96,768]{1,0:T(8,128)(2,1)}), bf16[768,768]{1,0:T(8,128)(2,1)}) %all-gather.8.cloned.1.call-update) | async-done | bytes 1179664 | tf_op jit(solution)/shard_map/all_gather | solution.py:109
  329.9 12.2 %convert_reduce_fusion = (f32[768]{0:T(1024)}, bf16[2048,768]{1,0:T(8,128)(2,1)S(1)}, bf16[2048,768]{1,0:T(8,128)(2,1)}) fusion(f32[2048,768]{1,0:T(8,128)} %fusion.89, f32[768]{0:T(1024)S(1)} %dynamic_slice.28, bf16[2048,768]{1,0:T(8,128)(2,1)} %constant_dynamic-update-slice_fusion, bf16[768,768]{1,0:T(8,128)(2,1)} %all-gather.8.cloned.1.call-done), kind=kOutput, calls=%fused_computation.57 | convolution fusion | flops 2455239936 | bytes 16914432 | tf_op jit(solution)/shard_map/dot_general | solution.py:185
  355.2 28.7 %reduce-scatter.17.cloned.1.call-done = bf16[512,768]{1,0:T(8,128)(2,1)} async-done(((bf16[2048,768]{1,0:T(8,128)(2,1)}), bf16[512,768]{1,0:T(8,128)(2,1)}) %reduce-scatter.17.cloned.1.call-update) | async-done | bytes 786448 | tf_op jit(solution)/shard_map/reduce_scatter | solution.py:212
  387.9 36.4 %reduce-scatter.15.cloned.1.call-done = bf16[512,768]{1,0:T(8,128)(2,1)} async-done(((bf16[2048,768]{1,0:T(8,128)(2,1)}), bf16[512,768]{1,0:T(8,128)(2,1)}) %reduce-scatter.15.cloned.1.call-update) | async-done | bytes 786448 | tf_op jit(solution)/shard_map/reduce_scatter | solution.py:188
  431.5 28.6 %all-gather.14.cloned.1.call-done = bf16[2048,768]{1,0:T(8,128)(2,1)} async-done(((bf16[512,768]{1,0:T(8,128)(2,1)}), bf16[2048,768]{1,0:T(8,128)(2,1)}) %all-gather.14.cloned.1.call-update) | async-done | bytes 3145744 | tf_op jit(solution)/shard_map/all_gather | solution.py:231
  463.9 157.7 %while.28 = (s32[]{:T(128)}, f32[2048,3,64]{0,2,1:T(8,128)}, f32[2048,3,64]{0,2,1:T(8,128)}, f32[4,512,3,64]{1,0,3,2:T(4,128)}, bf16[4,512,3,64]{1,3,2,0:T(8,128...) while((s32[]{:T(128)}, f32[2048,3,64]{0,2,1:T(8,128)}, ...), condition=%wide.region_18.19_spmd.clone, body=%wide.region_16.18_spmd.clone.sunk | while | flops 2053634560 | bytes 151972176 | solution.py:265
  493.4 8.6 dynamic_update_slice.44
  533.2 8.6 dynamic_update_slice.44
  573.1 8.6 dynamic_update_slice.44
  612.9 8.6 dynamic_update_slice.44
  669.1 23.5 %reduce-scatter.27.cloned.1.call-done = f32[96,192]{1,0:T(8,128)} async-done(((f32[768,192]{1,0:T(8,128)}), f32[96,192]{1,0:T(8,128)}) %reduce-scatter.27.cloned.1.call-update) | async-done | bytes 73744
  694.3 68.3 %reduce-scatter.25.cloned.1.call-done = f32[96,576]{1,0:T(8,128)} async-done(((f32[768,576]{1,0:T(8,128)}), f32[96,576]{1,0:T(8,128)}) %reduce-scatter.25.cloned.1.call-update) | async-done | bytes 221200
  764.5 37.7 %reduce-scatter.19.cloned.1.call-done = bf16[512,768]{1,0:T(8,128)(2,1)} async-done(((bf16[2048,768]{1,0:T(8,128)(2,1)}), bf16[512,768]{1,0:T(8,128)(2,1)}) %reduce-scatter.19.cloned.1.call-update) | async-done | bytes 786448 | tf_op jit(solution)/shard_map/reduce_scatter | solution.py:279
  804.8 41.5 %all-reduce = (f32[768]{0:T(1024)}, f32[768]{0:T(1024)}, f32[768]{0:T(1024)}, f32[3072]{0:T(1024)}, f32[768]{0:T(1024)}, /*index=5*/f32[2304]{0:T(1024)}) all-reduce(f32[768]{0:T(1024)S(1)} %get-tuple-element.311, f32[768]{0:T(1024)S(1)} %get-tuple-element.314, ...), channel_id=1, replica_groups=mesh['dp'=8,'tensor'=4] {'dp','tensor'}, use_global_device_ids=true, to_apply=%region_23.24 | all-reduce | flops 8448 | bytes 67584 | tf_op jit(solution)/shard_map/psum | solution.py:296
  849.5 26.8 %reduce-scatter.21.cloned.1.call-done = f32[96,768]{1,0:T(8,128)} async-done(((f32[768,768]{1,0:T(8,128)}), f32[96,768]{1,0:T(8,128)}) %reduce-scatter.21.cloned.1.call-update) | async-done | bytes 294928 | tf_op jit(solution)/shard_map/reduce_scatter | solution.py:293
  876.3 73.0 %reduce-scatter.23.cloned.1.call-done = f32[768,96]{0,1:T(8,128)} async-done(((f32[768,768]{0,1:T(8,128)}), f32[768,96]{0,1:T(8,128)}) %reduce-scatter.23.cloned.1.call-update) | async-done | bytes 294928 | tf_op jit(solution)/shard_map/reduce_scatter | solution.py:294
  (351 shorter events, 345.3 us)
Async XLA Ops:
  8.0 195.1 %copy-start = (f32[128,2304]{1,0:T(8,128)S(1)}, f32[128,2304]{1,0:T(8,128)}, u32[]{:S(2)}) copy-start(f32[128,2304]{1,0:T(8,128)} %param.32) | copy-start | bytes 3538948
  8.1 78.7 %all-gather.6.cloned.1.call-start = ((), (), s32[]{:S(2)}) async-start(), calls=%async_computation.8 | async-start | bytes 3932160 | tf_op jit(solution)/shard_map/all_gather | solution.py:116
  11.6 226.0 %reduce-scatter.13.cloned.1.call-start = ((), (), s32[]{:S(2)}) async-start(), calls=%async_computation.9 | async-start | bytes 3932160 | tf_op jit(solution)/shard_map/reduce_scatter | solution.py:150
  200.7 72.8 %all-gather.10.cloned.1.call-start = ((), (), s32[]{:S(2)}) async-start(), calls=%async_computation.11 | async-start | bytes 1327104 | tf_op jit(solution)/shard_map/all_gather | solution.py:110
  202.3 83.3 %all-gather.12.cloned.1.call-start = ((), (), s32[]{:S(2)}) async-start(), calls=%async_computation.13 | async-start | bytes 3932160 | tf_op jit(solution)/shard_map/all_gather | solution.py:197
  209.3 120.6 %all-gather.8.cloned.1.call-start = ((), (), s32[]{:S(2)}) async-start(), calls=%async_computation.10 | async-start | bytes 1327104 | tf_op jit(solution)/shard_map/all_gather | solution.py:109
  210.1 173.9 %reduce-scatter.17.cloned.1.call-start = ((), (), s32[]{:S(2)}) async-start(), calls=%async_computation.14 | async-start | bytes 3932160 | tf_op jit(solution)/shard_map/reduce_scatter | solution.py:212
  244.6 28.9 %collective-permute-start = (bf16[512,768]{1,0:T(8,128)(2,1)}, bf16[512,768]{1,0:T(8,128)(2,1)S(1)}, u32[]{:S(2)}, u32[]{:S(2)}) collective-permute-start(bf16[512,768]{1,0:T(8,128)(2,1)} %get-tuple-element.366), channel_id=1, source_target_pairs={{0,1},{1,2},{2,3},{3,0},{4,5},{5,6},{6,7},{7,4},{8,9},{9,10},{10,1... | collective-permute-start | bytes 2359304 | tf_op jit(solution)/shard_map/ppermute | solution.py:171
  244.6 49.4 %collective-permute-start.1 = (bf16[512,768]{1,0:T(8,128)(2,1)}, bf16[512,768]{1,0:T(8,128)(2,1)S(1)}, u32[]{:S(2)}, u32[]{:S(2)}) collective-permute-start(bf16[512,768]{1,0:T(8,128)(2,1)} %get-tuple-element.366), channel_id=1, source_target_pairs={{0,3},{1,0},{2,1},{3,2},{4,7},{5,4},{6,5},{7,6},{8,11},{9,8},{10,9... | collective-permute-start | bytes 2359304 | tf_op jit(solution)/shard_map/ppermute | solution.py:178
  273.5 21.5 %collective-permute-start.2 = (bf16[512,768]{1,0:T(8,128)(2,1)S(1)}, bf16[512,768]{1,0:T(8,128)(2,1)S(1)}, u32[]{:S(2)}, u32[]{:S(2)}) collective-permute-start(bf16[512,768]{1,0:T(8,128)(2,1)S(1)} %collective-permute-done), channel_id=1, source_target_pairs={{0,1},{1,2},{2,3},{3,0},{4,5},{5,6},{6,7},{7,4},{8,9},{9,10},{10,1... | collective-permute-start | bytes 2359304 | tf_op jit(solution)/shard_map/ppermute | solution.py:171
  347.7 76.5 %reduce-scatter.15.cloned.1.call-start = ((), (), s32[]{:S(2)}) async-start(), calls=%async_computation.12 | async-start | bytes 3932160 | tf_op jit(solution)/shard_map/reduce_scatter | solution.py:188
  355.2 104.9 %all-gather.14.cloned.1.call-start = ((), (), s32[]{:S(2)}) async-start(), calls=%async_computation.15 | async-start | bytes 3932160 | tf_op jit(solution)/shard_map/all_gather | solution.py:231
  431.5 261.2 %reduce-scatter.27.cloned.1.call-start = ((), (), s32[]{:S(2)}) async-start(), calls=%async_computation.21 | async-start | bytes 884736
  629.1 133.5 %reduce-scatter.25.cloned.1.call-start = ((), (), s32[]{:S(2)}) async-start(), calls=%async_computation.20 | async-start | bytes 2211840
  642.6 159.5 %reduce-scatter.19.cloned.1.call-start = ((), (), s32[]{:S(2)}) async-start(), calls=%async_computation.16 | async-start | bytes 3932160 | tf_op jit(solution)/shard_map/reduce_scatter | solution.py:279
  649.0 227.3 %reduce-scatter.21.cloned.1.call-start = ((), (), s32[]{:S(2)}) async-start(), calls=%async_computation.17 | async-start | bytes 2654208 | tf_op jit(solution)/shard_map/reduce_scatter | solution.py:293
  656.2 293.1 %reduce-scatter.23.cloned.1.call-start = ((), (), s32[]{:S(2)}) async-start(), calls=%async_computation.18 | async-start | bytes 2654208 | tf_op jit(solution)/shard_map/reduce_scatter | solution.py:294
  662.5 286.8 %all-reduce.3.cloned.1.call-start = ((), (), s32[]{:S(2)}) async-start(), calls=%async_computation.19 | async-start | bytes 2359296 | tf_op jit(solution)/shard_map/psum | solution.py:296
  666.8 135.3 %copy-start.9 = (f32[512,768]{1,0:T(8,128)S(1)}, f32[512,768]{1,0:T(8,128)}, u32[]{:S(2)}) copy-start(f32[512,768]{1,0:T(8,128)} %param.19) | copy-start | bytes 4718596
  666.8 135.3 %copy-start.42 = (f32[512]{0:T(512)S(1)}, f32[512]{0:T(512)}, u32[]{:S(2)}) copy-start(f32[512]{0:T(512)} %copy-done.41) | copy-start | bytes 6148
  666.9 135.3 %copy-start.44 = (f32[768]{0:T(1024)S(1)}, f32[768]{0:T(1024)}, u32[]{:S(2)}) copy-start(f32[768]{0:T(1024)} %param.23) | copy-start | bytes 9220
  666.9 135.3 %copy-start.46 = (f32[512]{0:T(512)S(1)}, f32[512]{0:T(512)}, u32[]{:S(2)}) copy-start(f32[512]{0:T(512)} %copy-done.45) | copy-start | bytes 6148
  669.1 135.6 %copy-start.48 = (f32[768]{0:T(1024)S(1)}, f32[768]{0:T(1024)}, u32[]{:S(2)}) copy-start(f32[768]{0:T(1024)} %get-tuple-element.310) | copy-start | bytes 9220
  669.1 135.6 %copy-start.49 = (f32[768]{0:T(1024)S(1)}, f32[768]{0:T(1024)}, u32[]{:S(2)}) copy-start(f32[768]{0:T(1024)} %get-tuple-element.363) | copy-start | bytes 9220
  (75 other events, 838.4 us)
Sparse Core Ops, SparseCore 0:
  11.7 31.2 all-gather.5
  200.8 36.7 reduce-scatter.12
  431.6 28.4 all-gather.13
  669.3 151.9 all-reduce.2
Sparse Core Ops, SparseCore 1:
  203.9 40.2 all-gather.9
  246.2 39.3 all-gather.11
  287.6 42.2 all-gather.7
  347.8 36.1 reduce-scatter.16
  386.5 37.7 reduce-scatter.14
  629.2 63.4 reduce-scatter.26
  696.0 66.5 reduce-scatter.24
  765.0 37.1 reduce-scatter.18
  806.1 70.1 reduce-scatter.20
  880.3 68.9 reduce-scatter.22
